TPU v7x, 256 devices: a whole 4x4x8 slice. The times are simulated.
256 devices in a mesh: bank: 16 (over z, core), zero: 16 (over y, x).
Axes of the slice: x: 4, y: 4, z: 8, core: 2. Of those that a mesh axis runs over, the one named last changes fastest.
Arguments:
- master_gate: float32 [64, 2048, 1408], P('bank', 'zero'), may hold values from -0.1875 to 0.1875
- master_up: float32 [64, 2048, 1408], P('bank', 'zero'), may hold values from -0.1875 to 0.1875
- master_down: float32 [64, 1408, 2048], P('bank', None, 'zero'), may hold values from -0.21875 to 0.21875
- router_weight: float32 [2048, 64], P('zero', 'bank'), may hold values from -0.125 to 0.125
- router_gain: float32 [2048], P('zero'), may hold values from 0.25 to 1.75
Outputs:
- final_gate: bfloat16 [64, 2048, 1408], P('bank', None, 'zero')
- final_up: bfloat16 [64, 2048, 1408], P('bank', None, 'zero')
- final_down: bfloat16 [64, 1408, 2048], P('bank', 'zero')
- scale_gate: float32 [64, 1408], P('bank', 'zero')
- scale_up: float32 [64, 1408], P('bank', 'zero')
- scale_down: float32 [64, 1408], P('bank', 'zero')
- serve_router: bfloat16 [2048, 64], replicated
All inputs are finite; a program needn't handle non-finite values. Where the computation divides by a largest or mean magnitude, that divisor is 1e-20 or more.
Results may differ from a plain program's by a relative error of at most 0.0013.
Values may be sent and summed in bfloat16 or wider, within the bound.
A program may use at most 64 MiB of HBM per device.

v0:
```python
import jax
import jax.numpy as jnp
from jax import lax
from jax.sharding import PartitionSpec as P

D_MODEL = 2048


def copy_for_each(x, axis):
    count = lax.axis_size(axis)
    return lax.all_to_all(jnp.broadcast_to(x[None], (count, *x.shape)), axis, 0, 0, tiled=True)


def taken_together(x, axis):
    return copy_for_each(x, axis).sum(axis=0)


def in_one(arrays, axis):
    vector, at, finished = (jnp.concatenate([a.reshape(-1) for a in arrays]), 0, [])
    total = taken_together(vector, axis)
    for a in arrays:
        finished.append(total[at : at + a.size].reshape(a.shape))
        at += a.size
    return tuple(finished)


def side_by_side(arrays, axis, split_dim, concat_dim, along):
    both = jnp.concatenate(arrays, axis=along)
    whole, at, finished = (
        lax.all_to_all(both, axis, split_axis=split_dim, concat_axis=concat_dim, tiled=True),
        0,
        [],
    )
    for a in arrays:
        finished.append(lax.slice_in_dim(whole, at, at + a.shape[along], axis=along))
        at += a.shape[along]
    return tuple(finished)


def laid_out(pieces, dim):
    shape = list(pieces.shape[1:])
    shape[dim] *= pieces.shape[0]
    return jnp.moveaxis(pieces, 0, dim).reshape(shape)


def gather_directly(x, axis, dim):
    pieces = copy_for_each(x, axis)
    return laid_out(pieces, dim)


def local(master_gate, master_up, master_down, router_weight, router_gain):
    total_gate, total_up, total_down = in_one(
        (
            jnp.sum(jnp.abs(master_gate), axis=1),
            jnp.sum(jnp.abs(master_up), axis=1),
            jnp.sum(jnp.abs(master_down), axis=2),
        ),
        "zero",
    )
    scale_gate = total_gate / D_MODEL
    scale_up = total_up / D_MODEL
    scale_down = total_down / D_MODEL
    narrow_gate, narrow_up, narrow_down = (
        (master_gate / jnp.expand_dims(scale_gate, 1)).astype(jnp.bfloat16),
        (master_up / jnp.expand_dims(scale_up, 1)).astype(jnp.bfloat16),
        (master_down / jnp.expand_dims(scale_down, 2)).astype(jnp.bfloat16),
    )
    final_gate, final_up = side_by_side((narrow_gate, narrow_up), "zero", 2, 1, 0)
    final_down = lax.all_to_all(narrow_down, "zero", split_axis=1, concat_axis=2, tiled=True)
    scale_gate = lax.dynamic_slice_in_dim(
        scale_gate, lax.axis_index("zero") * final_gate.shape[2], final_gate.shape[2], axis=1
    )
    scale_up = lax.dynamic_slice_in_dim(
        scale_up, lax.axis_index("zero") * final_up.shape[2], final_up.shape[2], axis=1
    )
    scale_down = lax.dynamic_slice_in_dim(
        scale_down, lax.axis_index("zero") * final_down.shape[1], final_down.shape[1], axis=1
    )
    part_router = (router_weight * router_gain[:, None]).astype(jnp.bfloat16)
    row_router = gather_directly(part_router, "zero", 0)
    serve_router = lax.all_gather(row_router, "bank", axis=1, tiled=True)
    return (final_gate, final_up, final_down, scale_gate, scale_up, scale_down, serve_router)


def solution(mesh):
    placed = (
        P("bank", "zero", None),
        P("bank", "zero", None),
        P("bank", None, "zero"),
        P("zero", "bank"),
        P("zero"),
    )
    return jax.shard_map(
        local,
        mesh=mesh,
        in_specs=placed,
        out_specs=(
            P("bank", None, "zero"),
            P("bank", None, "zero"),
            P("bank", "zero", None),
            P("bank", "zero"),
            P("bank", "zero"),
            P("bank", "zero"),
            P(),
        ),
        check_vma=False,
    )
```

profile of v0, /device:TPU:8, one launch (start us, length us, event | category | flops | bytes accessed | tf_op | source)
XLA Modules:
  0.0 124.2 jit_solution(8950060846199024515)
XLA Ops:
  0.6 2.2 %abs_reduce_fusion.2 = f32[4,1408]{1,0:T(4,128)S(1)} fusion(f32[4,128,1408]{2,1,0:T(8,128)} %param.5), kind=kLoop, calls=%fused_computation.4 | loop fusion | flops 1436160 | bytes 2906112 | tf_op jit(solution)/shard_map/reduce_sum | solution.py:54
  3.6 2.8 %abs_reduce_fusion = f32[4,1408]{1,0:T(4,128)S(1)} fusion(f32[4,1408,128]{2,1,0:T(8,128)} %param.7), kind=kLoop, calls=%fused_computation.2 | loop fusion | flops 1436160 | bytes 2906112 | tf_op jit(solution)/shard_map/reduce_sum | solution.py:56
  6.4 1.5 %broadcast_in_dim.4 = f32[16,1,16896]{2,1,0:T(1,128)} broadcast(f32[16896]{0:T(1024)S(1)} %pad_maximum_fusion.1), dimensions={2} | broadcast | bytes 1148928 | tf_op jit(solution)/shard_map/broadcast_in_dim | solution.py:11
  8.0 7.4 %all-to-all-start = ((f32[16,1,16896]{2,1,0:T(1,128)}), f32[16,1,16896]{2,1,0:T(1,128)}, u32[]{:S(2)}, u32[]{:S(2)}) async-start(f32[16,1,16896]{2,1,0:T(1,128)} %broadcast_in_dim.4), calls=%async_computation | async-start | bytes 2162688 | tf_op jit(solution)/shard_map/all_to_all | solution.py:11
  15.4 2.9 %copy.44 = f32[4,128,1408]{1,0,2:T(4,128)} copy(f32[4,128,1408]{2,1,0:T(8,128)S(1)} %copy-done) | data formatting | bytes 5767168 | tf_op args[0]
  18.2 4.6 %copy.46 = f32[4,128,1408]{1,0,2:T(4,128)} copy(f32[4,128,1408]{2,1,0:T(8,128)} %param.6) | data formatting | bytes 5767168 | tf_op args[1]
  22.9 7.5 %all-to-all-done = f32[16,1,16896]{2,1,0:T(1,128)} async-done(((f32[16,1,16896]{2,1,0:T(1,128)}), f32[16,1,16896]{2,1,0:T(1,128)}, u32[]{:S(2)}, u32[]{:S(2)}) %all-to-all-start) | async-done | bytes 1081376 | tf_op jit(solution)/shard_map/all_to_all | solution.py:11
  31.0 6.5 %all-to-all-start.3 = ((bf16[16,128,4]{1,2,0:T(4,128)(2,1)}), bf16[16,128,4]{1,2,0:T(4,128)(2,1)S(1)}, u32[]{:S(2)}, u32[]{:S(2)}) async-start(bf16[16,128,4]{1,2,0:T(4,128)(2,1)} %broadcast_in_dim.5), calls=%async_computation.3 | async-start | bytes 32768 | tf_op jit(solution)/shard_map/all_to_all | solution.py:11
  37.5 1.9 %reduce_sum.39 = f32[16896]{0:T(1024)S(1)} reduce(f32[16,1,16896]{2,1,0:T(1,128)} %all-to-all-done, f32[]{:T(128)} %constant.6.clone.1), dimensions={0,1}, to_apply=%region_3.0 | reduce | flops 253440 | bytes 1148932 | tf_op jit(solution)/shard_map/reduce_sum | solution.py:15
  39.5 1.2 copy.50
  40.6 7.7 %fusion = bf16[4,1408,128]{2,0,1:T(4,128)(2,1)} fusion(f32[4,1408,128]{2,1,0:T(8,128)S(1)} %copy-done.2, f32[4,1408]{0,1:T(8,128)} %copy.50), kind=kLoop, calls=%fused_computation.5 | loop fusion | flops 1441792 | bytes 4347904 | tf_op jit(solution)/shard_map/convert_element_type | solution.py:66
  48.4 1.2 copy.43
  49.6 1.2 copy.45
  50.7 7.3 %all-to-all-start.2 = ((bf16[4,1408,128]{2,0,1:T(4,128)(2,1)}), bf16[4,1408,128]{2,0,1:T(4,128)(2,1)}, u32[]{:S(2)}, u32[]{:S(2)}) async-start(bf16[4,1408,128]{2,0,1:T(4,128)(2,1)} %fusion), calls=%async_computation.2 | async-start | bytes 2883584 | tf_op jit(solution)/shard_map/all_to_all | solution.py:69
  58.0 6.6 %divide_convert_fusion = (bf16[4,128,1408]{1,0,2:T(4,128)(2,1)S(1)}, bf16[4,128,1408]{1,0,2:T(4,128)(2,1)S(1)}) fusion(f32[4,128,1408]{1,0,2:T(4,128)} %copy.46, f32[4,1408]{0,1:T(8,128)} %copy.45, f32[4,128,1408]{1,0,2:T(4,128)S(1)} %copy-done.3, f32[4,1408]{0,1:T(8,128)} %copy.43), kind=kLoop, calls=%fused_computation.6 | loop fusion | flops 2883584 | bytes 8695808 | tf_op jit(solution)/shard_map/convert_element_type | solution.py:65
  64.6 2.6 %pad_maximum_fusion = bf16[8,128,1408]{1,0,2:T(8,128)(2,1)} fusion(bf16[4,128,1408]{1,0,2:T(4,128)(2,1)S(1)} %get-tuple-element.12, bf16[4,128,1408]{1,0,2:T(4,128)(2,1)S(1)} %get-tuple-element.13), kind=kLoop, calls=%fused_computation | loop fusion | flops 5767168 | bytes 5767168 | tf_op jit(solution)/shard_map/concatenate | solution.py:28
  67.2 9.4 %all-to-all-done.2 = bf16[4,1408,128]{2,0,1:T(4,128)(2,1)} async-done(((bf16[4,1408,128]{2,0,1:T(4,128)(2,1)}), bf16[4,1408,128]{2,0,1:T(4,128)(2,1)}, u32[]{:S(2)}, u32[]{:S(2)}) %all-to-all-start.2) | async-done | bytes 1441824 | tf_op jit(solution)/shard_map/all_to_all | solution.py:69
  76.6 6.2 %all-to-all-start.1 = ((bf16[8,128,1408]{1,0,2:T(8,128)(2,1)}), bf16[8,128,1408]{1,0,2:T(8,128)(2,1)S(1)}, u32[]{:S(2)}, u32[]{:S(2)}) async-start(bf16[8,128,1408]{1,0,2:T(8,128)(2,1)} %pad_maximum_fusion), calls=%async_computation.1 | async-start | bytes 5767168 | tf_op jit(solution)/shard_map/all_to_all | solution.py:30
  82.8 20.7 %all-gather = bf16[16,4,2048]{2,1,0:T(4,128)(2,1)S(1)} all-gather(bf16[1,4,2048]{2,1,0:T(4,128)(2,1)S(1)} %bitcast.28), channel_id=1, replica_groups=mesh['bank'=16,'zero'=16] {'bank'}, dimensions={0}, use_global_device_ids=true | all-gather | bytes 278528 | tf_op jit(solution)/shard_map/all_gather | solution.py:81
  105.6 3.0 %copy.52 = bf16[4,88,16,128]{3,2,1,0:T(8,128)(2,1)} copy(bf16[4,88,16,128]{3,0,1,2:T(4,128)(2,1)} %bitcast.4) | data formatting | bytes 2883584 | tf_op jit(solution)/shard_map/all_to_all | solution.py:69
  108.6 3.5 %all_to_all.38 = bf16[4,88,2048]{2,1,0:T(8,128)(2,1)} reshape(bf16[4,88,16,128]{3,2,1,0:T(8,128)(2,1)} %copy.52) | data formatting | bytes 2883584 | tf_op jit(solution)/shard_map/all_to_all | solution.py:69
  112.1 8.6 %all-to-all-done.1 = bf16[8,128,1408]{1,0,2:T(8,128)(2,1)S(1)} async-done(((bf16[8,128,1408]{1,0,2:T(8,128)(2,1)}), bf16[8,128,1408]{1,0,2:T(8,128)(2,1)S(1)}, u32[]{:S(2)}, u32[]{:S(2)}) %all-to-all-start.1) | async-done | bytes 2883616 | tf_op jit(solution)/shard_map/all_to_all | solution.py:30
  121.3 1.5 %copy.64 = bf16[4,16,11,8,128]{4,3,1,2,0:T(8,128)(2,1)} copy(bf16[4,16,11,8,128]{4,3,2,1,0:T(8,128)(2,1)S(1)} %get-tuple-element.7) | data formatting | bytes 2883584 | tf_op jit(solution)/shard_map/slice | solution.py:35
  122.8 1.5 %copy.65 = bf16[4,16,11,8,128]{4,3,1,2,0:T(8,128)(2,1)} copy(bf16[4,16,11,8,128]{4,3,2,1,0:T(8,128)(2,1)S(1)} %get-tuple-element.8) | data formatting | bytes 2883584 | tf_op jit(solution)/shard_map/slice | solution.py:35
  (29 shorter events, 4.1 us)
Async XLA Ops:
  0.6 2.7 %copy-start.1 = (f32[4,128,1408]{2,1,0:T(8,128)S(1)}, f32[4,128,1408]{2,1,0:T(8,128)}, u32[]{:S(2)}) copy-start(f32[4,128,1408]{2,1,0:T(8,128)} %param.6) | copy-start | bytes 8650756
  3.6 11.8 %copy-start = (f32[4,128,1408]{2,1,0:T(8,128)S(1)}, f32[4,128,1408]{2,1,0:T(8,128)}, u32[]{:S(2)}) copy-start(f32[4,128,1408]{2,1,0:T(8,128)} %param.5) | copy-start | bytes 8650756
  8.0 22.4 %all-to-all-start = ((f32[16,1,16896]{2,1,0:T(1,128)}), f32[16,1,16896]{2,1,0:T(1,128)}, u32[]{:S(2)}, u32[]{:S(2)}) async-start(f32[16,1,16896]{2,1,0:T(1,128)} %broadcast_in_dim.4), calls=%async_computation | async-start | bytes 2162688 | tf_op jit(solution)/shard_map/all_to_all | solution.py:11
  18.2 4.7 %copy-start.4 = (f32[128,4]{0,1:T(4,128)S(1)}, f32[128,4]{0,1:T(4,128)}, u32[]{:S(2)}) copy-start(f32[128,4]{0,1:T(4,128)} %param.8) | copy-start | bytes 6148
  18.2 4.7 %copy-start.5 = (f32[128]{0:T(128)S(1)}, f32[128]{0:T(128)}, u32[]{:S(2)}) copy-start(f32[128]{0:T(128)} %param.9) | copy-start | bytes 1540
  18.2 22.4 %copy-start.2 = (f32[4,1408,128]{2,1,0:T(8,128)S(1)}, f32[4,1408,128]{2,1,0:T(8,128)}, u32[]{:S(2)}) copy-start(f32[4,1408,128]{2,1,0:T(8,128)} %param.7) | copy-start | bytes 8650756
  31.0 19.7 %all-to-all-start.3 = ((bf16[16,128,4]{1,2,0:T(4,128)(2,1)}), bf16[16,128,4]{1,2,0:T(4,128)(2,1)S(1)}, u32[]{:S(2)}, u32[]{:S(2)}) async-start(bf16[16,128,4]{1,2,0:T(4,128)(2,1)} %broadcast_in_dim.5), calls=%async_computation.3 | async-start | bytes 32768 | tf_op jit(solution)/shard_map/all_to_all | solution.py:11
  48.4 9.6 %copy-start.3 = (f32[4,128,1408]{1,0,2:T(4,128)S(1)}, f32[4,128,1408]{1,0,2:T(4,128)}, u32[]{:S(2)}) copy-start(f32[4,128,1408]{1,0,2:T(4,128)} %copy.44) | copy-start | bytes 8650756
  50.7 25.9 %all-to-all-start.2 = ((bf16[4,1408,128]{2,0,1:T(4,128)(2,1)}), bf16[4,1408,128]{2,0,1:T(4,128)(2,1)}, u32[]{:S(2)}, u32[]{:S(2)}) async-start(bf16[4,1408,128]{2,0,1:T(4,128)(2,1)} %fusion), calls=%async_computation.2 | async-start | bytes 2883584 | tf_op jit(solution)/shard_map/all_to_all | solution.py:69
  76.6 44.0 %all-to-all-start.1 = ((bf16[8,128,1408]{1,0,2:T(8,128)(2,1)}), bf16[8,128,1408]{1,0,2:T(8,128)(2,1)S(1)}, u32[]{:S(2)}, u32[]{:S(2)}) async-start(bf16[8,128,1408]{1,0,2:T(8,128)(2,1)} %pad_maximum_fusion), calls=%async_computation.1 | async-start | bytes 5767168 | tf_op jit(solution)/shard_map/all_to_all | solution.py:30
where the time goes:
time: 126 us; the launch traced here: 124 us
  starting transfers between devices  27.4 us (22%)
  local copies, waits for them, and re-layouts  25.8 us (20%)
  waiting for transfers between devices  25.5 us (20%)
  other arithmetic  24.1 us (19%)
  blocking collectives  20.7 us (16%)
    all_gather x1, blocking collectives, local(): serve_router = lax.all_gather(row_router, 'bank', axis=1, tiled=True)  20.7 us
    all_to_all x2, starting transfers between devices, copy_for_each(): lax.all_to_all(jnp.broadcast_to(x[None], (count, *x.shape)), axis, 0, 0,...  13.9 us
    all_to_all x1, waiting for transfers between devices, local(): lax.all_to_all(narrow_down, 'zero', split_axis=1, concat_axis=2, tiled=True)  9.43 us
    unnamed x16, local copies, waits for them, and re-layouts  8.94 us
    all_to_all x1, waiting for transfers between devices, side_by_side(): lax.all_to_all(both, axis, split_axis=split_dim, concat_axis=concat_dim,...  8.6 us
    convert_element_type x1, other arithmetic, local(): (master_down / jnp.expand_dims(scale_down, 2)).astype(jnp.bfloat16)  7.73 us
    all_to_all x2, waiting for transfers between devices, copy_for_each(): lax.all_to_all(jnp.broadcast_to(x[None], (count, *x.shape)), axis, 0, 0,...  7.51 us
    all_to_all x1, starting transfers between devices, local(): lax.all_to_all(narrow_down, 'zero', split_axis=1, concat_axis=2, tiled=True)  7.26 us
  transfers between devices with their start and end apart: 4, of which 3 were waited for; matrix products, arithmetic and copies ran while one was open for 28% of the time, Pallas kernels for 0%

commit v1 on v0

v1 whole, which is shorter than its diff:
```python
import functools

import jax
import jax.numpy as jnp
from jax import lax
from jax.experimental import pallas as pl
from jax.experimental.pallas import tpu as pltpu
from jax.sharding import PartitionSpec as P

MESH = pl.DeviceIdType.MESH
N = 16
D_MODEL = 2048
EXP = 4
WIDE = 1408
OWN = 128
PIECE = WIDE // N


def exchange_kernel(
    gate, up, down, weight, gain,
    out_gate, out_up, out_down, scales_ab, scales_c, router_rows,
    x, t, s, piece_a, piece_b, part_a, part_b, mine_a, mine_b, all_a, all_b,
    send, router_part, router_line,
    load_sem, rs_send, rs_recv, ag_send, ag_recv, out_send, out_recv, rz_send, rz_recv, rb_send, rb_recv,
):
    me = lax.axis_index("zero")
    bank = lax.axis_index("bank")

    def peer(k):
        y, xx = me // 4, me % 4
        return ((y + k // 4) % 4) * 4 + (xx + k % 4) % 4

    def bank_peer(k):
        return ((bank // 2 + k // 2) % 8) * 2 + (bank % 2 + k % 2) % 2

    def remote(src, dst, send_sem, recv_sem, to):
        return pltpu.make_async_remote_copy(
            src_ref=src, dst_ref=dst, send_sem=send_sem, recv_sem=recv_sem, device_id=to, device_id_type=MESH
        )

    loads = []
    for m in range(12):
        source = (gate, up, down)[m // 4].at[m % 4]
        target = x.at[m] if m < 8 else t.at[m]
        loads.append(pltpu.make_async_copy(source, target, load_sem.at[m]))
    for c in loads:
        c.start()

    barrier = pltpu.get_barrier_semaphore()

    @pl.loop(1, N)
    def _(k):
        pl.semaphore_signal(barrier, inc=1, device_id=(bank, peer(k)), device_id_type=MESH)
        pl.semaphore_signal(barrier, inc=1, device_id=(bank_peer(k), me), device_id_type=MESH)

    router_part[...] = (weight[...] * gain[...]).astype(jnp.bfloat16)
    column = pl.ds(pl.multiple_of(me * OWN, OWN), OWN)
    router_line[:, column] = router_part[...]

    for m in range(8):
        loads[m].wait()
        s[pl.ds(m, 1), pl.ds(0, WIDE)] = jnp.sum(jnp.abs(x[m]), axis=0, keepdims=True)
    s[:, pl.ds(WIDE, 128)] = jnp.zeros((8, 128), jnp.float32)
    for d in range(N):
        base = (PIECE * d) // 128 * 128
        both = s[:, pl.ds(base, 256)]
        shift = (256 - (PIECE * d - base)) % 256
        piece_a[d] = (pltpu.roll(both, shift, 1) if shift else both)[:, :128]
    pl.semaphore_wait(barrier, 2 * (N - 1))

    def rs_copy(k, piece, part, which):
        to = peer(k)
        return remote(piece.at[to], part.at[me], rs_send.at[which, k], rs_recv.at[which, k], (bank, to))

    def rz_copy(k):
        return remote(router_part, router_line.at[:, column], rz_send.at[k], rz_recv.at[k], (bank, peer(k)))

    @pl.loop(1, N)
    def _(k):
        rs_copy(k, piece_a, part_a, 0).start()

    part_a[me] = piece_a[me]

    eye = lax.broadcasted_iota(jnp.int32, (PIECE, OWN), 0) == lax.broadcasted_iota(jnp.int32, (PIECE, OWN), 1)
    for m in range(8, 12):
        loads[m].wait()

    @pl.loop(0, N)
    def _(d):
        rows = pl.ds(pl.multiple_of(d * PIECE, 8), PIECE)
        for e in range(EXP):
            total = jnp.sum(jnp.abs(t[8 + e, rows, :]), axis=1, keepdims=True)
            piece_b[d, pl.ds(e, 1), :] = jnp.sum(jnp.where(eye, total, 0.0), axis=0, keepdims=True)
        piece_b[d, pl.ds(4, 4), :] = jnp.zeros((4, OWN), jnp.float32)

    @pl.loop(1, N)
    def _(k):
        rs_copy(k, piece_b, part_b, 1).start()
        rz_copy(k).start()

    part_b[me] = piece_b[me]

    def turn(lo, hi):
        for m in range(lo, hi):
            for c in range(WIDE // 128):
                t[m, pl.ds(c * 128, 128), :] = x[m, :, pl.ds(c * 128, 128)].T

    def ag_copy(k, mine, whole, which):
        return remote(mine, whole.at[me], ag_send.at[which, k], ag_recv.at[which, k], (bank, peer(k)))

    def reduce_and_spread(piece, part, mine, whole, which):
        @pl.loop(1, N)
        def _(k):
            rs_copy(k, piece, part, which).wait_recv()

        total = part[0]
        for d in range(1, N):
            total = total + part[d]
        scale = total / D_MODEL
        mine[...] = scale
        whole[me] = scale

        @pl.loop(1, N)
        def _(k):
            ag_copy(k, mine, whole, which).start()

        return scale

    turn(0, 4)
    scale_a = reduce_and_spread(piece_a, part_a, mine_a, all_a, 0)
    scales_ab[...] = scale_a
    scale_b = reduce_and_spread(piece_b, part_b, mine_b, all_b, 1)
    scales_c[...] = scale_b

    @pl.loop(1, N)
    def _(k):
        rz_copy(k).wait_recv()

    def rb_copy(k):
        return remote(router_line, router_rows.at[bank], rb_send.at[k], rb_recv.at[k], (bank_peer(k), me))

    @pl.loop(1, N)
    def _(k):
        rb_copy(k).start()

    router_rows[bank] = router_line[...]

    turn(4, 8)

    @pl.loop(1, N)
    def _(k):
        ag_copy(k, mine_a, all_a, 0).wait_recv()
        ag_copy(k, mine_b, all_b, 1).wait_recv()

    outs = (out_gate, out_up, out_down)

    def scaled(to, m):
        row = (all_a if m < 8 else all_b)[to, pl.ds(m % 8, 1), :]
        factor = jnp.sum(jnp.where(eye, 1.0 / row, 0.0), axis=1, keepdims=True)
        rows = pl.ds(pl.multiple_of(to * PIECE, 8), PIECE)
        return (t[m, rows, :] * factor).astype(jnp.bfloat16)

    def out_copy(k, i):
        return remote(
            send.at[k, pl.ds(4 * i, 4)], outs[i].at[:, :, column], out_send.at[i, k], out_recv.at[i, k], (bank, peer(k))
        )

    @pl.loop(1, N)
    def _(k):
        to = peer(k)
        for i in range(3):
            for e in range(EXP):
                send[k, 4 * i + e] = scaled(to, 4 * i + e)
            out_copy(k, i).start()

    for m in range(12):
        outs[m // 4][m % 4, :, column] = scaled(me, m)

    @pl.loop(1, N)
    def _(k):
        for i in range(3):
            out_copy(k, i).wait()
        rb_copy(k).wait()
        rz_copy(k).wait_send()
        for which, (piece, part, mine, whole) in enumerate(
            ((piece_a, part_a, mine_a, all_a), (piece_b, part_b, mine_b, all_b))
        ):
            rs_copy(k, piece, part, which).wait_send()
            ag_copy(k, mine, whole, which).wait_send()


def exchange(gate, up, down, weight, gain):
    f32, bf16 = jnp.float32, jnp.bfloat16
    vmem, anywhere = pl.BlockSpec(memory_space=pltpu.VMEM), pl.BlockSpec(memory_space=pl.ANY)
    big = jax.ShapeDtypeStruct((EXP, PIECE, D_MODEL), bf16)
    small = jax.ShapeDtypeStruct((8, 128), f32)
    return pl.pallas_call(
        exchange_kernel,
        name="exchange",
        out_shape=(big, big, big, small, small, jax.ShapeDtypeStruct((N, EXP, D_MODEL), bf16)),
        in_specs=[anywhere, anywhere, anywhere, vmem, vmem],
        out_specs=(vmem,) * 6,
        scratch_shapes=[
            pltpu.VMEM((8, OWN, WIDE), f32),
            pltpu.VMEM((12, WIDE, OWN), f32),
            pltpu.VMEM((8, WIDE + 128), f32),
            pltpu.VMEM((N, 8, 128), f32),
            pltpu.VMEM((N, 8, 128), f32),
            pltpu.VMEM((N, 8, 128), f32),
            pltpu.VMEM((N, 8, 128), f32),
            pltpu.VMEM((8, 128), f32),
            pltpu.VMEM((8, 128), f32),
            pltpu.VMEM((N, 8, 128), f32),
            pltpu.VMEM((N, 8, 128), f32),
            pltpu.VMEM((N, 12, PIECE, OWN), bf16),
            pltpu.VMEM((EXP, OWN), bf16),
            pltpu.VMEM((EXP, D_MODEL), bf16),
            pltpu.SemaphoreType.DMA((12,)),
            pltpu.SemaphoreType.DMA((2, N)),
            pltpu.SemaphoreType.DMA((2, N)),
            pltpu.SemaphoreType.DMA((2, N)),
            pltpu.SemaphoreType.DMA((2, N)),
            pltpu.SemaphoreType.DMA((3, N)),
            pltpu.SemaphoreType.DMA((3, N)),
            pltpu.SemaphoreType.DMA((N,)),
            pltpu.SemaphoreType.DMA((N,)),
            pltpu.SemaphoreType.DMA((N,)),
            pltpu.SemaphoreType.DMA((N,)),
        ],
        compiler_params=pltpu.CompilerParams(
            collective_id=0, has_side_effects=True, vmem_limit_bytes=48 * 1024 * 1024
        ),
    )(gate, up, down, weight, gain)


def finish_kernel(a, b, c, scales_ab, scales_c, rows, fa, fb, fc, sa, sb, sc, fr, router, sem):
    copies = [
        pltpu.make_async_copy(src, dst, sem.at[i]) for i, (src, dst) in enumerate(((a, fa), (b, fb), (c, fc)))
    ]
    for c_ in copies:
        c_.start()
    sa[...] = scales_ab[pl.ds(0, 4), pl.ds(0, PIECE)]
    sb[...] = scales_ab[pl.ds(4, 4), pl.ds(0, PIECE)]
    sc[...] = scales_c[pl.ds(0, 4), pl.ds(0, PIECE)]
    for i in range(N):
        router[pl.ds(4 * i, 4), :] = rows[i]
    last = pltpu.make_async_copy(router, fr, sem.at[3])
    last.start()
    for c_ in copies:
        c_.wait()
    last.wait()


def finish(*parts):
    f32, bf16 = jnp.float32, jnp.bfloat16
    vmem, anywhere = pl.BlockSpec(memory_space=pltpu.VMEM), pl.BlockSpec(memory_space=pl.ANY)
    big = jax.ShapeDtypeStruct((EXP, PIECE, D_MODEL), bf16)
    small = jax.ShapeDtypeStruct((EXP, PIECE), f32)
    return pl.pallas_call(
        finish_kernel,
        name="finish",
        out_shape=(big, big, big, small, small, small, jax.ShapeDtypeStruct((N * EXP, D_MODEL), bf16)),
        in_specs=[vmem] * 6,
        out_specs=(anywhere,) * 3 + (vmem,) * 3 + (anywhere,),
        scratch_shapes=[pltpu.VMEM((N * EXP, D_MODEL), bf16), pltpu.SemaphoreType.DMA((4,))],
        compiler_params=pltpu.CompilerParams(vmem_limit_bytes=16 * 1024 * 1024),
    )(*parts)


def local(master_gate, master_up, master_down, router_weight, router_gain):
    parts = exchange(master_gate, master_up, master_down, router_weight.T, router_gain.reshape(1, OWN))
    fa, fb, fc, sa, sb, sc, fr = finish(*parts)
    return (fa.transpose(0, 2, 1), fb.transpose(0, 2, 1), fc, sa, sb, sc, fr.T)


def solution(mesh):
    placed = (
        P("bank", "zero", None),
        P("bank", "zero", None),
        P("bank", None, "zero"),
        P("zero", "bank"),
        P("zero"),
    )
    return jax.shard_map(
        local,
        mesh=mesh,
        in_specs=placed,
        out_specs=(
            P("bank", None, "zero"),
            P("bank", None, "zero"),
            P("bank", "zero", None),
            P("bank", "zero"),
            P("bank", "zero"),
            P("bank", "zero"),
            P(),
        ),
        check_vma=False,
    )
```

time: 126 us -> 93.3 us (0.74)
  Pallas kernels: 0 us -> 90.2 us
  starting transfers between devices: 27.4 us -> 0 us
  waiting for transfers between devices: 25.5 us -> 0 us
  local copies, waits for them, and re-layouts: 25.8 us -> 1.33 us
  other arithmetic: 24.1 us -> 0 us
  blocking collectives: 20.7 us -> 0 us
    pallas_call x0 -> x2, Pallas kernels: none -> 90.2 us  [the longest x1 87.5 us: exchange(): pl.pallas_call(exchange_kernel, name='exchange', out_shape=(big, big, big...]
    all_to_all x4 -> x0, starting transfers between devices: 27.4 us -> none  [the longest x2 13.9 us: copy_for_each(): lax.all_to_all(jnp.broadcast_to(x[None], (count, *x.shape)), axis, 0, 0,...]
    all_to_all x4 -> x0, waiting for transfers between devices: 25.5 us -> none  [the longest x1 9.43 us: local(): lax.all_to_all(narrow_down, 'zero', split_axis=1, concat_axis=2, tiled=True)]
    all_gather x1 -> x0, blocking collectives: 20.7 us -> none  [local(): serve_router = lax.all_gather(row_router, 'bank', axis=1, tiled=True)]
    convert_element_type x3 -> x0, other arithmetic: 14.3 us -> none  [the longest x1 7.73 us: local(): (master_down / jnp.expand_dims(scale_down, 2)).astype(jnp.bfloat16)]
    unnamed x16 -> x4, local copies, waits for them, and re-layouts: 8.94 us -> 1.33 us
    reduce_sum x4 -> x0, other arithmetic: 7.16 us -> none  [the longest x1 2.79 us: local(): jnp.sum(jnp.abs(master_down), axis=2)]
    all_to_all x3 -> x0, local copies, waits for them, and re-layouts: 6.87 us -> none  [the longest x2 6.5 us: local(): lax.all_to_all(narrow_down, 'zero', split_axis=1, concat_axis=2, tiled=True)]
  transfers between devices with their start and end apart: 4 -> 0, of which waited for: 3 -> 0; matrix products, arithmetic and copies ran while one was open for 28% -> 0% of each run, Pallas kernels for 0% -> 0%
where the time goes in v1:
time: 93.3 us; the launch traced here: 92.2 us
  Pallas kernels  90.2 us (97%)
  local copies, waits for them, and re-layouts  1.33 us (1%)
    pallas_call x1, Pallas kernels, exchange(): pl.pallas_call(exchange_kernel, name='exchange', out_shape=(big, big, big...  87.5 us
    pallas_call x1, Pallas kernels, finish(): pl.pallas_call(finish_kernel, name='finish', out_shape=(big, big, big, sm...  2.75 us

profile of v1, /device:TPU:8, one launch (start us, length us, event | category | flops | bytes accessed | tf_op | source)
XLA Modules:
  0.0 92.2 jit_solution(1108517141072464381)
XLA Ops:
  0.6 0.0 copy-start
  0.6 0.7 copy-done
  1.3 0.0 copy-start.1
  1.3 0.7 copy-done.1
  2.0 87.5 %exchange.1 = (bf16[4,88,2048]{2,1,0:T(8,128)(2,1)S(1)}, bf16[4,88,2048]{2,1,0:T(8,128)(2,1)S(1)}, bf16[4,88,2048]{2,1,0:T(8,128)(2,1)S(1)}, f32[8,128]{1,0:T(8,...) custom-call(f32[4,128,1408]{2,1,0:T(8,128)} %gate.1, f32[4,128,1408]{2,1,0:T(8,128)} %up.1, ...), custom_call_target="tpu_custom_call" | custom-call | tf_op jit(solution)/shard_map/exchange/pallas_call | solution.py:197
  89.5 2.8 %finish.1 = (bf16[4,88,2048]{2,1,0:T(8,128)(2,1)}, bf16[4,88,2048]{2,1,0:T(8,128)(2,1)}, bf16[4,88,2048]{2,1,0:T(8,128)(2,1)}, f32[4,88]{1,0:T(4,128)}, f32[4,88...) custom-call(bf16[4,88,2048]{2,1,0:T(8,128)(2,1)S(1)} %get-tuple-element.20.a, ...), custom_call_target="tpu_custom_call" | custom-call | tf_op jit(solution)/shard_map/finish/pallas_call | solution.py:259
Async XLA Ops:
  0.6 0.7 copy-start
  1.3 0.7 copy-start.1

commit v2 on v1

--- a/solution.py
+++ b/solution.py
@@ -14,14 +14,16 @@
 WIDE = 1408
 OWN = 128
 PIECE = WIDE // N
+PEERS = ((1, 1), (3, 3), (1, 3), (3, 1), (1, 0), (3, 0), (0, 1), (0, 3), (1, 2), (3, 2), (2, 1), (2, 3), (2, 2), (0, 2), (2, 0))
+ORDER = tuple(4 * a + b for a, b in PEERS)
 
 
 def exchange_kernel(
-    gate, up, down, weight, gain,
+    gate, up, down, weight_hbm, gain_hbm,
     out_gate, out_up, out_down, scales_ab, scales_c, router_rows,
     x, t, s, piece_a, piece_b, part_a, part_b, mine_a, mine_b, all_a, all_b,
-    send, router_part, router_line,
-    load_sem, rs_send, rs_recv, ag_send, ag_recv, out_send, out_recv, rz_send, rz_recv, rb_send, rb_recv,
+    send, router_part, router_line, weight, gain,
+    load_sem, rs_send, rs_recv, ag_send, ag_recv, out_send, out_recv, rz_send, rz_recv, rb_send, rb_recv, later,
 ):
     me = lax.axis_index("zero")
     bank = lax.axis_index("bank")
@@ -31,13 +33,14 @@
         return ((y + k // 4) % 4) * 4 + (xx + k % 4) % 4
 
     def bank_peer(k):
-        return ((bank // 2 + k // 2) % 8) * 2 + (bank % 2 + k % 2) % 2
+        return (bank + k) % N
 
     def remote(src, dst, send_sem, recv_sem, to):
         return pltpu.make_async_remote_copy(
             src_ref=src, dst_ref=dst, send_sem=send_sem, recv_sem=recv_sem, device_id=to, device_id_type=MESH
         )
 
+    column = pl.ds(pl.multiple_of(me * OWN, OWN), OWN)
     loads = []
     for m in range(12):
         source = (gate, up, down)[m // 4].at[m % 4]
@@ -48,15 +51,21 @@
 
     barrier = pltpu.get_barrier_semaphore()
 
-    @pl.loop(1, N)
-    def _(k):
+    for k in ORDER:
         pl.semaphore_signal(barrier, inc=1, device_id=(bank, peer(k)), device_id_type=MESH)
-        pl.semaphore_signal(barrier, inc=1, device_id=(bank_peer(k), me), device_id_type=MESH)
-
-    router_part[...] = (weight[...] * gain[...]).astype(jnp.bfloat16)
-    column = pl.ds(pl.multiple_of(me * OWN, OWN), OWN)
-    router_line[:, column] = router_part[...]
-
+
+    @pl.loop(1, N)
+    def _(j):
+        @pl.when(bank + j < N)
+        def _():
+            pl.semaphore_signal(barrier, inc=1, device_id=(bank + j, me), device_id_type=MESH)
+
+    small_loads = [
+        pltpu.make_async_copy(weight_hbm, weight, load_sem.at[12]),
+        pltpu.make_async_copy(gain_hbm, gain, load_sem.at[13]),
+    ]
+    for c in small_loads:
+        c.start()
     for m in range(8):
         loads[m].wait()
         s[pl.ds(m, 1), pl.ds(0, WIDE)] = jnp.sum(jnp.abs(x[m]), axis=0, keepdims=True)
@@ -66,7 +75,7 @@
         both = s[:, pl.ds(base, 256)]
         shift = (256 - (PIECE * d - base)) % 256
         piece_a[d] = (pltpu.roll(both, shift, 1) if shift else both)[:, :128]
-    pl.semaphore_wait(barrier, 2 * (N - 1))
+    pl.semaphore_wait(barrier, N - 1 + bank)
 
     def rs_copy(k, piece, part, which):
         to = peer(k)
@@ -75,8 +84,7 @@
     def rz_copy(k):
         return remote(router_part, router_line.at[:, column], rz_send.at[k], rz_recv.at[k], (bank, peer(k)))
 
-    @pl.loop(1, N)
-    def _(k):
+    for k in ORDER:
         rs_copy(k, piece_a, part_a, 0).start()
 
     part_a[me] = piece_a[me]
@@ -93,9 +101,13 @@
             piece_b[d, pl.ds(e, 1), :] = jnp.sum(jnp.where(eye, total, 0.0), axis=0, keepdims=True)
         piece_b[d, pl.ds(4, 4), :] = jnp.zeros((4, OWN), jnp.float32)
 
-    @pl.loop(1, N)
-    def _(k):
+    for c in small_loads:
+        c.wait()
+    router_part[...] = (weight[...] * gain[...]).astype(jnp.bfloat16)
+    router_line[:, column] = router_part[...]
+    for k in ORDER:
         rs_copy(k, piece_b, part_b, 1).start()
+    for k in ORDER:
         rz_copy(k).start()
 
     part_b[me] = piece_b[me]
@@ -120,8 +132,7 @@
         mine[...] = scale
         whole[me] = scale
 
-        @pl.loop(1, N)
-        def _(k):
+        for k in ORDER:
             ag_copy(k, mine, whole, which).start()
 
         return scale
@@ -133,17 +144,10 @@
     scales_c[...] = scale_b
 
     @pl.loop(1, N)
-    def _(k):
-        rz_copy(k).wait_recv()
-
-    def rb_copy(k):
-        return remote(router_line, router_rows.at[bank], rb_send.at[k], rb_recv.at[k], (bank_peer(k), me))
-
-    @pl.loop(1, N)
-    def _(k):
-        rb_copy(k).start()
-
-    router_rows[bank] = router_line[...]
+    def _(j):
+        @pl.when(bank >= j)
+        def _():
+            pl.semaphore_signal(later, inc=1, device_id=(bank - j, me), device_id_type=MESH)
 
     turn(4, 8)
 
@@ -165,13 +169,29 @@
             send.at[k, pl.ds(4 * i, 4)], outs[i].at[:, :, column], out_send.at[i, k], out_recv.at[i, k], (bank, peer(k))
         )
 
-    @pl.loop(1, N)
-    def _(k):
+    for k in ORDER:
         to = peer(k)
         for i in range(3):
             for e in range(EXP):
                 send[k, 4 * i + e] = scaled(to, 4 * i + e)
             out_copy(k, i).start()
+
+    @pl.loop(1, N)
+    def _(k):
+        rz_copy(k).wait_recv()
+
+    def rb_copy(k):
+        return remote(router_line, router_rows.at[bank], rb_send.at[k], rb_recv.at[k], (bank_peer(k), me))
+
+    @pl.when(bank < N - 1)
+    def _():
+        pl.semaphore_wait(later, N - 1 - bank)
+
+    @pl.loop(1, N)
+    def _(k):
+        rb_copy(k).start()
+
+    router_rows[bank] = router_line[...]
 
     for m in range(12):
         outs[m // 4][m % 4, :, column] = scaled(me, m)
@@ -198,7 +218,7 @@
         exchange_kernel,
         name="exchange",
         out_shape=(big, big, big, small, small, jax.ShapeDtypeStruct((N, EXP, D_MODEL), bf16)),
-        in_specs=[anywhere, anywhere, anywhere, vmem, vmem],
+        in_specs=[anywhere] * 5,
         out_specs=(vmem,) * 6,
         scratch_shapes=[
             pltpu.VMEM((8, OWN, WIDE), f32),
@@ -215,7 +235,9 @@
             pltpu.VMEM((N, 12, PIECE, OWN), bf16),
             pltpu.VMEM((EXP, OWN), bf16),
             pltpu.VMEM((EXP, D_MODEL), bf16),
-            pltpu.SemaphoreType.DMA((12,)),
+            pltpu.VMEM((EXP, OWN), f32),
+            pltpu.VMEM((1, OWN), f32),
+            pltpu.SemaphoreType.DMA((14,)),
             pltpu.SemaphoreType.DMA((2, N)),
             pltpu.SemaphoreType.DMA((2, N)),
             pltpu.SemaphoreType.DMA((2, N)),
@@ -226,6 +248,7 @@
             pltpu.SemaphoreType.DMA((N,)),
             pltpu.SemaphoreType.DMA((N,)),
             pltpu.SemaphoreType.DMA((N,)),
+            pltpu.SemaphoreType.REGULAR,
         ],
         compiler_params=pltpu.CompilerParams(
             collective_id=0, has_side_effects=True, vmem_limit_bytes=48 * 1024 * 1024

time: 93.3 us -> 76.9 us (0.82)
  Pallas kernels: 90.2 us -> 74.8 us
    pallas_call x1, Pallas kernels: 87.5 us -> 72 us  [exchange(): pl.pallas_call(exchange_kernel, name='exchange', out_shape=(big, big, big...]
where the time goes in v2:
time: 76.9 us; the launch traced here: 76.7 us
  Pallas kernels  74.8 us (97%)
  local copies, waits for them, and re-layouts  1.33 us (2%)
    pallas_call x1, Pallas kernels, exchange(): pl.pallas_call(exchange_kernel, name='exchange', out_shape=(big, big, big...  72 us
    pallas_call x1, Pallas kernels, finish(): pl.pallas_call(finish_kernel, name='finish', out_shape=(big, big, big, sm...  2.75 us

profile of v2, /device:TPU:8, one launch (start us, length us, event | category | flops | bytes accessed | tf_op | source)
XLA Modules:
  0.0 76.7 jit_solution(698274818889150226)
XLA Ops:
  0.6 0.0 copy-start
  0.6 0.7 copy-done
  1.3 0.0 copy-start.1
  1.3 0.7 copy-done.1
  2.0 72.0 %exchange.1 = (bf16[4,88,2048]{2,1,0:T(8,128)(2,1)S(1)}, bf16[4,88,2048]{2,1,0:T(8,128)(2,1)S(1)}, bf16[4,88,2048]{2,1,0:T(8,128)(2,1)S(1)}, f32[8,128]{1,0:T(8,...) custom-call(f32[4,128,1408]{2,1,0:T(8,128)} %gate.1, f32[4,128,1408]{2,1,0:T(8,128)} %up.1, ...), custom_call_target="tpu_custom_call" | custom-call | tf_op jit(solution)/shard_map/exchange/pallas_call | solution.py:217
  74.0 2.8 %finish.1 = (bf16[4,88,2048]{2,1,0:T(8,128)(2,1)}, bf16[4,88,2048]{2,1,0:T(8,128)(2,1)}, bf16[4,88,2048]{2,1,0:T(8,128)(2,1)}, f32[4,88]{1,0:T(4,128)}, f32[4,88...) custom-call(bf16[4,88,2048]{2,1,0:T(8,128)(2,1)S(1)} %get-tuple-element.20.a, ...), custom_call_target="tpu_custom_call" | custom-call | tf_op jit(solution)/shard_map/finish/pallas_call | solution.py:282
Async XLA Ops:
  0.6 0.7 copy-start
  1.3 0.7 copy-start.1

commit v3 on v2

v3 whole, which is shorter than its diff:
```python
import functools

import jax
import jax.numpy as jnp
from jax import lax
from jax.experimental import pallas as pl
from jax.experimental.pallas import tpu as pltpu
from jax.sharding import PartitionSpec as P

MESH = pl.DeviceIdType.MESH
N = 16
D_MODEL = 2048
EXP = 4
WIDE = 1408
OWN = 128
PIECE = WIDE // N
PEERS = ((1, 1), (3, 3), (1, 3), (3, 1), (1, 0), (3, 0), (0, 1), (0, 3), (1, 2), (3, 2), (2, 1), (2, 3), (2, 2), (0, 2), (2, 0))
RAW = 1
RAW_CUTS = (0, 40, 88)
ORDER = tuple(4 * a + b for a, b in PEERS)


def exchange_kernel(
    gate, up, down, weight_hbm, gain_hbm,
    out_gate, out_up, out_down, scales, router_rows,
    x, t, s, piece, part, mine, whole, send, router_part, router_line, weight, gain, raw_in,
    load_sem, rs_send, rs_recv, ag_send, ag_recv, out_send, out_recv, rz_send, rz_recv, rb_send, rb_recv,
    raw_send, raw_recv, later,
):
    me = lax.axis_index("zero")
    bank = lax.axis_index("bank")
    outs = (out_gate, out_up, out_down)
    column = pl.ds(pl.multiple_of(me * OWN, OWN), OWN)

    def peer(k):
        y, xx = me // 4, me % 4
        return ((y + k // 4) % 4) * 4 + (xx + k % 4) % 4

    def remote(src, dst, send_sem, recv_sem, to):
        return pltpu.make_async_remote_copy(
            src_ref=src, dst_ref=dst, send_sem=send_sem, recv_sem=recv_sem, device_id=to, device_id_type=MESH
        )

    loads = {}
    for m in range(12):
        source = (gate, up, down)[m // 4].at[m % 4]
        target = x.at[m] if m < 8 else t.at[m]
        loads[m] = pltpu.make_async_copy(source, target, load_sem.at[m])
    loads[12] = pltpu.make_async_copy(weight_hbm, weight, load_sem.at[12])
    loads[13] = pltpu.make_async_copy(gain_hbm, gain, load_sem.at[13])
    for c in loads.values():
        c.start()

    barrier = pltpu.get_barrier_semaphore()
    for k in ORDER:
        pl.semaphore_signal(barrier, inc=1, device_id=(bank, peer(k)), device_id_type=MESH)

    @pl.loop(1, N)
    def _(j):
        @pl.when(bank + j < N)
        def _():
            pl.semaphore_signal(barrier, inc=1, device_id=(bank + j, me), device_id_type=MESH)

    def rs_copy(k, i):
        to = peer(k)
        return remote(piece.at[i, to], part.at[i, me], rs_send.at[i, k], rs_recv.at[i, k], (bank, to))

    def ag_copy(k, i):
        return remote(mine.at[i], whole.at[i, me], ag_send.at[i, k], ag_recv.at[i, k], (bank, peer(k)))

    def raw_copy(k, e, half):
        to = peer(k)
        lo, hi = RAW_CUTS[half], RAW_CUTS[half + 1]
        return remote(
            t.at[8 + e, pl.ds(pl.multiple_of(to * PIECE + lo, 8), hi - lo), :],
            raw_in.at[k, pl.ds(e * PIECE + lo, hi - lo), :],
            raw_send.at[e, half, k], raw_recv.at[e, half, k], (bank, to),
        )

    def raw_spread(half):
        if half == 0:
            for e in range(RAW):
                loads[8 + e].wait()
        for e in range(RAW):
            if RAW_CUTS[half + 1] > RAW_CUTS[half]:
                for k in ORDER:
                    raw_copy(k, e, half).start()

    def rz_copy(k):
        return remote(router_part, router_line.at[:, column], rz_send.at[k], rz_recv.at[k], (bank, peer(k)))

    s[:, pl.ds(WIDE, 128)] = jnp.zeros((8, 128), jnp.float32)

    def lane_sums(i):
        for m in range(4 * i, 4 * i + 4):
            loads[m].wait()
            s[pl.ds(m, 1), pl.ds(0, WIDE)] = jnp.sum(jnp.abs(x[m]), axis=0, keepdims=True)
        for d in range(N):
            base = (PIECE * d) // 128 * 128
            both = s[:, pl.ds(base, 256)]
            shift = (256 - (PIECE * d - base)) % 256
            moved = pltpu.roll(both, shift, 1) if shift else both
            piece[i, d] = moved[4 * i : 4 * i + 4, :128]

    eye = lax.broadcasted_iota(jnp.int32, (PIECE, OWN), 0) == lax.broadcasted_iota(jnp.int32, (PIECE, OWN), 1)

    def row_sums():
        for m in range(8 + RAW, 12):
            loads[m].wait()

        @pl.loop(0, N)
        def _(d):
            rows = pl.ds(pl.multiple_of(d * PIECE, 8), PIECE)
            for e in range(EXP):
                total = jnp.sum(jnp.abs(t[8 + e, rows, :]), axis=1, keepdims=True)
                piece[2, d, pl.ds(e, 1), :] = jnp.sum(jnp.where(eye, total, 0.0), axis=0, keepdims=True)

    def rs_spread(i):
        for k in ORDER:
            rs_copy(k, i).start()
        part[i, me] = piece[i, me]

    lane_sums(0)
    lane_sums(1)
    pl.semaphore_wait(barrier, N - 1 + bank)
    rs_spread(0)
    rs_spread(1)
    raw_spread(0)
    row_sums()
    rs_spread(2)

    loads[12].wait()
    loads[13].wait()
    router_part[...] = (weight[...] * gain[...]).astype(jnp.bfloat16)
    router_line[:, column] = router_part[...]
    for k in ORDER:
        rz_copy(k).start()

    @pl.loop(1, N)
    def _(j):
        @pl.when(bank >= j)
        def _():
            pl.semaphore_signal(later, inc=1, device_id=(bank - j, me), device_id_type=MESH)

    def turn(i):
        for m in range(4 * i, 4 * i + 4):
            for c in range(WIDE // 128):
                t[m, pl.ds(c * 128, 128), :] = x[m, :, pl.ds(c * 128, 128)].T

    def reduce_and_spread(i):
        @pl.loop(1, N)
        def _(k):
            rs_copy(k, i).wait_recv()

        total = part[i, 0]
        for d in range(1, N):
            total = total + part[i, d]
        scale = total / D_MODEL
        mine[i] = scale
        whole[i, me] = scale
        scales[i] = scale
        for k in ORDER:
            ag_copy(k, i).start()

    def upright(row):
        return jnp.sum(jnp.where(eye, 1.0 / row, 0.0), axis=1, keepdims=True)

    def scaled(to, m):
        factor = upright(whole[m // 4, to, pl.ds(m % 4, 1), :])
        rows = pl.ds(pl.multiple_of(to * PIECE, 8), PIECE)
        return (t[m, rows, :] * factor).astype(jnp.bfloat16)

    def out_copy(k, i):
        lo = RAW if i == 2 else 0
        return remote(
            send.at[k, pl.ds(4 * i + lo, 4 - lo)], outs[i].at[pl.ds(lo, 4 - lo), :, column],
            out_send.at[i, k], out_recv.at[i, k], (bank, peer(k)),
        )

    def out_spread(i):
        @pl.loop(1, N)
        def _(k):
            ag_copy(k, i).wait_recv()

        for k in ORDER:
            to = peer(k)
            for e in range(RAW if i == 2 else 0, EXP):
                send[k, 4 * i + e] = scaled(to, 4 * i + e)
            out_copy(k, i).start()

    turn(0)
    reduce_and_spread(0)
    reduce_and_spread(1)
    raw_spread(1)
    reduce_and_spread(2)
    out_spread(0)
    turn(1)
    out_spread(1)
    out_spread(2)

    @pl.loop(1, N)
    def _(k):
        rz_copy(k).wait_recv()

    def rb_copy(k):
        return remote(
            router_line, router_rows.at[bank], rb_send.at[k], rb_recv.at[k], ((bank + k) % N, me)
        )

    @pl.when(bank < N - 1)
    def _():
        pl.semaphore_wait(later, N - 1 - bank)

    @pl.loop(1, N)
    def _(k):
        rb_copy(k).start()

    router_rows[bank] = router_line[...]
    for m in range(12):
        outs[m // 4][m % 4, :, column] = scaled(me, m)

    for e in range(RAW):
        factor = upright(mine[2, pl.ds(e, 1), :])

        @pl.loop(1, N)
        def _(k):
            for half in range(2):
                if RAW_CUTS[half + 1] > RAW_CUTS[half]:
                    raw_copy(k, e, half).wait_recv()
            source = ((me // 4 + 4 - k // 4) % 4) * 4 + (me % 4 + 4 - k % 4) % 4
            block = raw_in[k, pl.ds(e * PIECE, PIECE), :] * factor
            out_down[e, :, pl.ds(pl.multiple_of(source * OWN, OWN), OWN)] = block.astype(jnp.bfloat16)

    @pl.loop(1, N)
    def _(k):
        for i in range(3):
            out_copy(k, i).wait()
            rs_copy(k, i).wait_send()
            ag_copy(k, i).wait_send()
        rb_copy(k).wait()
        rz_copy(k).wait_send()
        for e in range(RAW):
            for half in range(2):
                if RAW_CUTS[half + 1] > RAW_CUTS[half]:
                    raw_copy(k, e, half).wait_send()


def exchange(gate, up, down, weight, gain):
    f32, bf16 = jnp.float32, jnp.bfloat16
    vmem, anywhere = pl.BlockSpec(memory_space=pltpu.VMEM), pl.BlockSpec(memory_space=pl.ANY)
    big = jax.ShapeDtypeStruct((EXP, PIECE, D_MODEL), bf16)
    return pl.pallas_call(
        exchange_kernel,
        name="exchange",
        out_shape=(big, big, big, jax.ShapeDtypeStruct((3, EXP, 128), f32), jax.ShapeDtypeStruct((N, EXP, D_MODEL), bf16)),
        in_specs=[anywhere] * 5,
        out_specs=(vmem,) * 5,
        scratch_shapes=[
            pltpu.VMEM((8, OWN, WIDE), f32),
            pltpu.VMEM((12, WIDE, OWN), f32),
            pltpu.VMEM((8, WIDE + 128), f32),
            pltpu.VMEM((3, N, EXP, 128), f32),
            pltpu.VMEM((3, N, EXP, 128), f32),
            pltpu.VMEM((3, EXP, 128), f32),
            pltpu.VMEM((3, N, EXP, 128), f32),
            pltpu.VMEM((N, 12, PIECE, OWN), bf16),
            pltpu.VMEM((EXP, OWN), bf16),
            pltpu.VMEM((EXP, D_MODEL), bf16),
            pltpu.VMEM((EXP, OWN), f32),
            pltpu.VMEM((1, OWN), f32),
            pltpu.VMEM((N, max(RAW, 1) * PIECE, OWN), f32),
            pltpu.SemaphoreType.DMA((14,)),
        ]
        + [pltpu.SemaphoreType.DMA((3, N))] * 6
        + [pltpu.SemaphoreType.DMA((N,))] * 4
        + [pltpu.SemaphoreType.DMA((max(RAW, 1), 2, N))] * 2
        + [pltpu.SemaphoreType.REGULAR],
        compiler_params=pltpu.CompilerParams(
            collective_id=0, has_side_effects=True, vmem_limit_bytes=48 * 1024 * 1024
        ),
    )(gate, up, down, weight, gain)


def finish_kernel(a, b, c, scales, rows, fa, fb, fc, sa, sb, sc, fr, router, sem):
    copies = [
        pltpu.make_async_copy(src, dst, sem.at[i]) for i, (src, dst) in enumerate(((a, fa), (b, fb), (c, fc)))
    ]
    for c_ in copies:
        c_.start()
    sa[...] = scales[0, :, pl.ds(0, PIECE)]
    sb[...] = scales[1, :, pl.ds(0, PIECE)]
    sc[...] = scales[2, :, pl.ds(0, PIECE)]
    for i in range(N):
        router[pl.ds(4 * i, 4), :] = rows[i]
    last = pltpu.make_async_copy(router, fr, sem.at[3])
    last.start()
    for c_ in copies:
        c_.wait()
    last.wait()


def finish(*parts):
    f32, bf16 = jnp.float32, jnp.bfloat16
    vmem, anywhere = pl.BlockSpec(memory_space=pltpu.VMEM), pl.BlockSpec(memory_space=pl.ANY)
    big = jax.ShapeDtypeStruct((EXP, PIECE, D_MODEL), bf16)
    small = jax.ShapeDtypeStruct((EXP, PIECE), f32)
    return pl.pallas_call(
        finish_kernel,
        name="finish",
        out_shape=(big, big, big, small, small, small, jax.ShapeDtypeStruct((N * EXP, D_MODEL), bf16)),
        in_specs=[vmem] * 5,
        out_specs=(anywhere,) * 3 + (vmem,) * 3 + (anywhere,),
        scratch_shapes=[pltpu.VMEM((N * EXP, D_MODEL), bf16), pltpu.SemaphoreType.DMA((4,))],
        compiler_params=pltpu.CompilerParams(vmem_limit_bytes=16 * 1024 * 1024),
    )(*parts)


def local(master_gate, master_up, master_down, router_weight, router_gain):
    parts = exchange(master_gate, master_up, master_down, router_weight.T, router_gain.reshape(1, OWN))
    fa, fb, fc, sa, sb, sc, fr = finish(*parts)
    return (fa.transpose(0, 2, 1), fb.transpose(0, 2, 1), fc, sa, sb, sc, fr.T)


def solution(mesh):
    placed = (
        P("bank", "zero", None),
        P("bank", "zero", None),
        P("bank", None, "zero"),
        P("zero", "bank"),
        P("zero"),
    )
    return jax.shard_map(
        local,
        mesh=mesh,
        in_specs=placed,
        out_specs=(
            P("bank", None, "zero"),
            P("bank", None, "zero"),
            P("bank", "zero", None),
            P("bank", "zero"),
            P("bank", "zero"),
            P("bank", "zero"),
            P(),
        ),
        check_vma=False,
    )
```

time: 76.9 us -> 69.8 us (0.908); the launches traced: 76.7 us -> 68.8 us
  Pallas kernels: 74.8 us -> 66.8 us
    pallas_call x1, Pallas kernels: 72 us -> 64.1 us  [exchange(): pl.pallas_call(exchange_kernel, name='exchange', out_shape=(big, big, big...]
where the time goes in v3:
time: 69.8 us; the launch traced here: 68.8 us
  Pallas kernels  66.8 us (96%)
  local copies, waits for them, and re-layouts  1.33 us (2%)
    pallas_call x1, Pallas kernels, exchange(): pl.pallas_call(exchange_kernel, name='exchange', out_shape=(big, big, big...  64.1 us
    pallas_call x1, Pallas kernels, finish(): pl.pallas_call(finish_kernel, name='finish', out_shape=(big, big, big, sm...  2.75 us

profile of v3, /device:TPU:8, one launch (start us, length us, event | category | flops | bytes accessed | tf_op | source)
XLA Modules:
  0.0 68.8 jit_solution(2823526553039339524)
XLA Ops:
  0.6 0.0 copy-start
  0.6 0.7 copy-done
  1.3 0.0 copy-start.1
  1.3 0.7 copy-done.1
  2.0 64.1 %exchange.1 = (bf16[4,88,2048]{2,1,0:T(8,128)(2,1)S(1)}, bf16[4,88,2048]{2,1,0:T(8,128)(2,1)S(1)}, bf16[4,88,2048]{2,1,0:T(8,128)(2,1)S(1)}, f32[3,4,128]{2,1,0:T(4,128)S(1)}, bf16[16,4,2048]{2,1,0:T(4,128)(2,1)S(1)}) custom-call(f32[4,128,1408]{2,1,0:T(8,128)} %gate.1, f32[4,128,1408]{2,1,0:T(8,128)} %up.1, f32[4,1408,128]{2,1,0:T(8,128)} %down.1, ...), custom_call_target="tpu_custom_call" | custom-call | tf_op jit(solution)/shard_map/exchange/pallas_call | solution.py:252
  66.1 2.7 %finish.1 = (bf16[4,88,2048]{2,1,0:T(8,128)(2,1)}, bf16[4,88,2048]{2,1,0:T(8,128)(2,1)}, bf16[4,88,2048]{2,1,0:T(8,128)(2,1)}, f32[4,88]{1,0:T(4,128)}, f32[4,88...) custom-call(bf16[4,88,2048]{2,1,0:T(8,128)(2,1)S(1)} %get-tuple-element.19.a, ...), custom_call_target="tpu_custom_call" | custom-call | tf_op jit(solution)/shard_map/finish/pallas_call | solution.py:307
Async XLA Ops:
  0.6 0.7 copy-start
  1.3 0.7 copy-start.1

commit v4 on v3

--- a/solution.py
+++ b/solution.py
@@ -15,21 +15,23 @@
 OWN = 128
 PIECE = WIDE // N
 PEERS = ((1, 1), (3, 3), (1, 3), (3, 1), (1, 0), (3, 0), (0, 1), (0, 3), (1, 2), (3, 2), (2, 1), (2, 3), (2, 2), (0, 2), (2, 0))
-RAW = 1
-RAW_CUTS = (0, 40, 88)
+RAW_CUTS = (0, 40, 64)
+RAW_END = RAW_CUTS[2]
 ORDER = tuple(4 * a + b for a, b in PEERS)
+FAR_FIRST = ORDER
+LAST_ORDER = ORDER
 
 
 def exchange_kernel(
     gate, up, down, weight_hbm, gain_hbm,
-    out_gate, out_up, out_down, scales, router_rows,
-    x, t, s, piece, part, mine, whole, send, router_part, router_line, weight, gain, raw_in,
+    out_gate, out_up, out_down, scale_gate, scale_up, scale_down, router,
+    router_rows, x, t, s, piece, part, mine, whole, send, router_part, router_line, weight, gain, raw_in,
     load_sem, rs_send, rs_recv, ag_send, ag_recv, out_send, out_recv, rz_send, rz_recv, rb_send, rb_recv,
     raw_send, raw_recv, later,
 ):
     me = lax.axis_index("zero")
     bank = lax.axis_index("bank")
-    outs = (out_gate, out_up, out_down)
+    outs, scales = (out_gate, out_up, out_down), (scale_gate, scale_up, scale_down)
     column = pl.ds(pl.multiple_of(me * OWN, OWN), OWN)
 
     def peer(k):
@@ -68,23 +70,20 @@
     def ag_copy(k, i):
         return remote(mine.at[i], whole.at[i, me], ag_send.at[i, k], ag_recv.at[i, k], (bank, peer(k)))
 
-    def raw_copy(k, e, half):
+    halves = [h for h in range(2) if RAW_CUTS[h + 1] > RAW_CUTS[h]]
+
+    def raw_copy(k, half):
         to = peer(k)
         lo, hi = RAW_CUTS[half], RAW_CUTS[half + 1]
         return remote(
-            t.at[8 + e, pl.ds(pl.multiple_of(to * PIECE + lo, 8), hi - lo), :],
-            raw_in.at[k, pl.ds(e * PIECE + lo, hi - lo), :],
-            raw_send.at[e, half, k], raw_recv.at[e, half, k], (bank, to),
+            t.at[8, pl.ds(pl.multiple_of(to * PIECE + lo, 8), hi - lo), :], raw_in.at[k, pl.ds(lo, hi - lo), :],
+            raw_send.at[half, k], raw_recv.at[half, k], (bank, to),
         )
 
     def raw_spread(half):
-        if half == 0:
-            for e in range(RAW):
-                loads[8 + e].wait()
-        for e in range(RAW):
-            if RAW_CUTS[half + 1] > RAW_CUTS[half]:
-                for k in ORDER:
-                    raw_copy(k, e, half).start()
+        if half in halves:
+            for k in ORDER:
+                raw_copy(k, half).start()
 
     def rz_copy(k):
         return remote(router_part, router_line.at[:, column], rz_send.at[k], rz_recv.at[k], (bank, peer(k)))
@@ -105,7 +104,7 @@
     eye = lax.broadcasted_iota(jnp.int32, (PIECE, OWN), 0) == lax.broadcasted_iota(jnp.int32, (PIECE, OWN), 1)
 
     def row_sums():
-        for m in range(8 + RAW, 12):
+        for m in range(9, 12):
             loads[m].wait()
 
         @pl.loop(0, N)
@@ -116,7 +115,7 @@
                 piece[2, d, pl.ds(e, 1), :] = jnp.sum(jnp.where(eye, total, 0.0), axis=0, keepdims=True)
 
     def rs_spread(i):
-        for k in ORDER:
+        for k in FAR_FIRST:
             rs_copy(k, i).start()
         part[i, me] = piece[i, me]
 
@@ -125,6 +124,7 @@
     pl.semaphore_wait(barrier, N - 1 + bank)
     rs_spread(0)
     rs_spread(1)
+    loads[8].wait()
     raw_spread(0)
     row_sums()
     rs_spread(2)
@@ -158,35 +158,47 @@
         scale = total / D_MODEL
         mine[i] = scale
         whole[i, me] = scale
-        scales[i] = scale
-        for k in ORDER:
+        scales[i][...] = scale[:, :PIECE]
+        for k in FAR_FIRST:
             ag_copy(k, i).start()
 
     def upright(row):
         return jnp.sum(jnp.where(eye, 1.0 / row, 0.0), axis=1, keepdims=True)
 
-    def scaled(to, m):
-        factor = upright(whole[m // 4, to, pl.ds(m % 4, 1), :])
-        rows = pl.ds(pl.multiple_of(to * PIECE, 8), PIECE)
+    def scaled(to, m, lo=0):
+        factor = upright(whole[m // 4, to, pl.ds(m % 4, 1), :])[lo:]
+        rows = pl.ds(pl.multiple_of(to * PIECE + lo, 8), PIECE - lo)
         return (t[m, rows, :] * factor).astype(jnp.bfloat16)
 
-    def out_copy(k, i):
-        lo = RAW if i == 2 else 0
-        return remote(
-            send.at[k, pl.ds(4 * i + lo, 4 - lo)], outs[i].at[pl.ds(lo, 4 - lo), :, column],
-            out_send.at[i, k], out_recv.at[i, k], (bank, peer(k)),
-        )
+    def out_copies(k, i):
+        first = 1 if i == 2 and RAW_END else 0
+        copies = [
+            remote(
+                send.at[k, pl.ds(4 * i + first, 4 - first)], outs[i].at[pl.ds(first, 4 - first), :, column],
+                out_send.at[i, k], out_recv.at[i, k], (bank, peer(k)),
+            )
+        ]
+        if first and RAW_END < PIECE:
+            rest = pl.ds(RAW_END, PIECE - RAW_END)
+            copies.append(
+                remote(
+                    send.at[k, 8, rest, :], out_down.at[0, rest, column],
+                    out_send.at[3, k], out_recv.at[3, k], (bank, peer(k)),
+                )
+            )
+        return copies
 
     def out_spread(i):
-        @pl.loop(1, N)
-        def _(k):
-            ag_copy(k, i).wait_recv()
-
-        for k in ORDER:
+        for k in LAST_ORDER if i == 2 else ORDER:
             to = peer(k)
-            for e in range(RAW if i == 2 else 0, EXP):
-                send[k, 4 * i + e] = scaled(to, 4 * i + e)
-            out_copy(k, i).start()
+            back = (4 - k // 4) % 4 * 4 + (4 - k % 4) % 4
+            ag_copy(back, i).wait_recv()
+            for e in range(EXP):
+                lo = RAW_END if i == 2 and e == 0 else 0
+                if lo < PIECE:
+                    send[k, 4 * i + e, pl.ds(lo, PIECE - lo), :] = scaled(to, 4 * i + e, lo)
+            for c in out_copies(k, i):
+                c.start()
 
     turn(0)
     reduce_and_spread(0)
@@ -219,43 +231,49 @@
     for m in range(12):
         outs[m // 4][m % 4, :, column] = scaled(me, m)
 
-    for e in range(RAW):
-        factor = upright(mine[2, pl.ds(e, 1), :])
+    if RAW_END:
+        own = upright(mine[2, pl.ds(0, 1), :])[:RAW_END]
 
         @pl.loop(1, N)
         def _(k):
-            for half in range(2):
-                if RAW_CUTS[half + 1] > RAW_CUTS[half]:
-                    raw_copy(k, e, half).wait_recv()
+            for half in halves:
+                raw_copy(k, half).wait_recv()
             source = ((me // 4 + 4 - k // 4) % 4) * 4 + (me % 4 + 4 - k % 4) % 4
-            block = raw_in[k, pl.ds(e * PIECE, PIECE), :] * factor
-            out_down[e, :, pl.ds(pl.multiple_of(source * OWN, OWN), OWN)] = block.astype(jnp.bfloat16)
+            block = raw_in[k, pl.ds(0, RAW_END), :] * own
+            out_down[0, pl.ds(0, RAW_END), pl.ds(pl.multiple_of(source * OWN, OWN), OWN)] = block.astype(jnp.bfloat16)
+
+    @pl.loop(1, N)
+    def _(k):
+        rb_copy(k).wait()
+
+    for b in range(N):
+        router[pl.ds(EXP * b, EXP), :] = router_rows[b]
 
     @pl.loop(1, N)
     def _(k):
         for i in range(3):
-            out_copy(k, i).wait()
             rs_copy(k, i).wait_send()
             ag_copy(k, i).wait_send()
-        rb_copy(k).wait()
+            for c in out_copies(k, i):
+                c.wait()
         rz_copy(k).wait_send()
-        for e in range(RAW):
-            for half in range(2):
-                if RAW_CUTS[half + 1] > RAW_CUTS[half]:
-                    raw_copy(k, e, half).wait_send()
+        for half in halves:
+            raw_copy(k, half).wait_send()
 
 
 def exchange(gate, up, down, weight, gain):
     f32, bf16 = jnp.float32, jnp.bfloat16
-    vmem, anywhere = pl.BlockSpec(memory_space=pltpu.VMEM), pl.BlockSpec(memory_space=pl.ANY)
+    vmem = pl.BlockSpec(memory_space=pltpu.VMEM)
     big = jax.ShapeDtypeStruct((EXP, PIECE, D_MODEL), bf16)
+    small = jax.ShapeDtypeStruct((EXP, PIECE), f32)
     return pl.pallas_call(
         exchange_kernel,
         name="exchange",
-        out_shape=(big, big, big, jax.ShapeDtypeStruct((3, EXP, 128), f32), jax.ShapeDtypeStruct((N, EXP, D_MODEL), bf16)),
-        in_specs=[anywhere] * 5,
-        out_specs=(vmem,) * 5,
+        out_shape=(big, big, big, small, small, small, jax.ShapeDtypeStruct((N * EXP, D_MODEL), bf16)),
+        in_specs=[pl.BlockSpec(memory_space=pltpu.HBM)] * 5,
+        out_specs=(vmem,) * 7,
         scratch_shapes=[
+            pltpu.VMEM((N, EXP, D_MODEL), bf16),
             pltpu.VMEM((8, OWN, WIDE), f32),
             pltpu.VMEM((12, WIDE, OWN), f32),
             pltpu.VMEM((8, WIDE + 128), f32),
@@ -268,12 +286,13 @@
             pltpu.VMEM((EXP, D_MODEL), bf16),
             pltpu.VMEM((EXP, OWN), f32),
             pltpu.VMEM((1, OWN), f32),
-            pltpu.VMEM((N, max(RAW, 1) * PIECE, OWN), f32),
+            pltpu.VMEM((N, PIECE, OWN), f32),
             pltpu.SemaphoreType.DMA((14,)),
         ]
-        + [pltpu.SemaphoreType.DMA((3, N))] * 6
+        + [pltpu.SemaphoreType.DMA((3, N))] * 4
+        + [pltpu.SemaphoreType.DMA((4, N))] * 2
         + [pltpu.SemaphoreType.DMA((N,))] * 4
-        + [pltpu.SemaphoreType.DMA((max(RAW, 1), 2, N))] * 2
+        + [pltpu.SemaphoreType.DMA((2, N))] * 2
         + [pltpu.SemaphoreType.REGULAR],
         compiler_params=pltpu.CompilerParams(
             collective_id=0, has_side_effects=True, vmem_limit_bytes=48 * 1024 * 1024
@@ -281,42 +300,33 @@
     )(gate, up, down, weight, gain)
 
 
-def finish_kernel(a, b, c, scales, rows, fa, fb, fc, sa, sb, sc, fr, router, sem):
-    copies = [
-        pltpu.make_async_copy(src, dst, sem.at[i]) for i, (src, dst) in enumerate(((a, fa), (b, fb), (c, fc)))
-    ]
-    for c_ in copies:
-        c_.start()
-    sa[...] = scales[0, :, pl.ds(0, PIECE)]
-    sb[...] = scales[1, :, pl.ds(0, PIECE)]
-    sc[...] = scales[2, :, pl.ds(0, PIECE)]
-    for i in range(N):
-        router[pl.ds(4 * i, 4), :] = rows[i]
-    last = pltpu.make_async_copy(router, fr, sem.at[3])
-    last.start()
-    for c_ in copies:
-        c_.wait()
-    last.wait()
+def finish_kernel(*refs):
+    sem = refs[-1]
+    copies = [pltpu.make_async_copy(refs[i], refs[7 + i], sem.at[i]) for i in range(7)]
+    for c in copies:
+        c.start()
+    for c in copies:
+        c.wait()
 
 
 def finish(*parts):
-    f32, bf16 = jnp.float32, jnp.bfloat16
     vmem, anywhere = pl.BlockSpec(memory_space=pltpu.VMEM), pl.BlockSpec(memory_space=pl.ANY)
-    big = jax.ShapeDtypeStruct((EXP, PIECE, D_MODEL), bf16)
-    small = jax.ShapeDtypeStruct((EXP, PIECE), f32)
     return pl.pallas_call(
         finish_kernel,
         name="finish",
-        out_shape=(big, big, big, small, small, small, jax.ShapeDtypeStruct((N * EXP, D_MODEL), bf16)),
-        in_specs=[vmem] * 5,
-        out_specs=(anywhere,) * 3 + (vmem,) * 3 + (anywhere,),
-        scratch_shapes=[pltpu.VMEM((N * EXP, D_MODEL), bf16), pltpu.SemaphoreType.DMA((4,))],
+        out_shape=tuple(jax.ShapeDtypeStruct(p.shape, p.dtype) for p in parts),
+        in_specs=[vmem] * 7,
+        out_specs=(anywhere,) * 7,
+        scratch_shapes=[pltpu.SemaphoreType.DMA((7,))],
         compiler_params=pltpu.CompilerParams(vmem_limit_bytes=16 * 1024 * 1024),
     )(*parts)
 
 
 def local(master_gate, master_up, master_down, router_weight, router_gain):
-    parts = exchange(master_gate, master_up, master_down, router_weight.T, router_gain.reshape(1, OWN))
+    router_weight, router_gain = (
+        pltpu.with_memory_space_constraint(a, pltpu.HBM) for a in (router_weight.T, router_gain.reshape(1, OWN))
+    )
+    parts = exchange(master_gate, master_up, master_down, router_weight, router_gain)
     fa, fb, fc, sa, sb, sc, fr = finish(*parts)
     return (fa.transpose(0, 2, 1), fb.transpose(0, 2, 1), fc, sa, sb, sc, fr.T)
 

time: 69.8 us -> 67.4 us (0.966)
  local copies, waits for them, and re-layouts: 1.33 us -> 0 us
  Pallas kernels: 66.8 us -> 65.7 us
    unnamed x4 -> x0, local copies, waits for them, and re-layouts: 1.33 us -> none
where the time goes in v4:
time: 67.4 us; the launch traced here: 66.4 us
  Pallas kernels  65.7 us (97%)
    pallas_call x1, Pallas kernels, exchange(): pl.pallas_call(exchange_kernel, name='exchange', out_shape=(big, big, big...  63.5 us
    pallas_call x1, Pallas kernels, finish(): pl.pallas_call(finish_kernel, name='finish', out_shape=tuple((jax.ShapeDt...  2.2 us

profile of v4, /device:TPU:8, one launch (start us, length us, event | category | flops | bytes accessed | tf_op | source)
XLA Modules:
  0.0 66.4 jit_solution(8509663026282594789)
XLA Ops:
  0.6 63.5 %exchange.1 = (bf16[4,88,2048]{2,1,0:T(8,128)(2,1)S(1)}, bf16[4,88,2048]{2,1,0:T(8,128)(2,1)S(1)}, bf16[4,88,2048]{2,1,0:T(8,128)(2,1)S(1)}, f32[4,88]{1,0:T(4,1...) custom-call(f32[4,128,1408]{2,1,0:T(8,128)} %gate.1, f32[4,128,1408]{2,1,0:T(8,128)} %up.1, ...), custom_call_target="tpu_custom_call" | custom-call | tf_op jit(solution)/shard_map/exchange/pallas_call | solution.py:269
  64.2 2.2 %finish.1 = (bf16[4,88,2048]{2,1,0:T(8,128)(2,1)}, bf16[4,88,2048]{2,1,0:T(8,128)(2,1)}, bf16[4,88,2048]{2,1,0:T(8,128)(2,1)}, f32[4,88]{1,0:T(4,128)}, f32[4,88...) custom-call(bf16[4,88,2048]{2,1,0:T(8,128)(2,1)S(1)} %get-tuple-element.21.refs_0_, ...), custom_call_target="tpu_custom_call" | custom-call | tf_op jit(solution)/shard_map/finish/pallas_call | solution.py:314

commit v5 on v4

--- a/solution.py
+++ b/solution.py
@@ -204,8 +204,8 @@
     reduce_and_spread(0)
     reduce_and_spread(1)
     raw_spread(1)
+    out_spread(0)
     reduce_and_spread(2)
-    out_spread(0)
     turn(1)
     out_spread(1)
     out_spread(2)

time: 67.4 us -> 67.5 us (level); the launches traced: 66.4 us -> 67.3 us
  Pallas kernels: 65.7 us -> 66.6 us
    pallas_call x1, Pallas kernels: 63.5 us -> 64.4 us  [exchange(): pl.pallas_call(exchange_kernel, name='exchange', out_shape=(big, big, big...]
where the time goes in v5:
time: 67.5 us; the launch traced here: 67.3 us
  Pallas kernels  66.6 us (99%)
    pallas_call x1, Pallas kernels, exchange(): pl.pallas_call(exchange_kernel, name='exchange', out_shape=(big, big, big...  64.4 us
    pallas_call x1, Pallas kernels, finish(): pl.pallas_call(finish_kernel, name='finish', out_shape=tuple((jax.ShapeDt...  2.2 us

profile of v5, /device:TPU:8, one launch (start us, length us, event | category | flops | bytes accessed | tf_op | source)
XLA Modules:
  0.0 67.3 jit_solution(4240012502887134419)
XLA Ops:
  0.6 64.4 %exchange.1 = (bf16[4,88,2048]{2,1,0:T(8,128)(2,1)S(1)}, bf16[4,88,2048]{2,1,0:T(8,128)(2,1)S(1)}, bf16[4,88,2048]{2,1,0:T(8,128)(2,1)S(1)}, f32[4,88]{1,0:T(4,1...) custom-call(f32[4,128,1408]{2,1,0:T(8,128)} %gate.1, f32[4,128,1408]{2,1,0:T(8,128)} %up.1, ...), custom_call_target="tpu_custom_call" | custom-call | tf_op jit(solution)/shard_map/exchange/pallas_call | solution.py:269
  65.1 2.2 %finish.1 = (bf16[4,88,2048]{2,1,0:T(8,128)(2,1)}, bf16[4,88,2048]{2,1,0:T(8,128)(2,1)}, bf16[4,88,2048]{2,1,0:T(8,128)(2,1)}, f32[4,88]{1,0:T(4,128)}, f32[4,88...) custom-call(bf16[4,88,2048]{2,1,0:T(8,128)(2,1)S(1)} %get-tuple-element.21.refs_0_, ...), custom_call_target="tpu_custom_call" | custom-call | tf_op jit(solution)/shard_map/finish/pallas_call | solution.py:314
